TPU v7x, 32 devices: a whole 2x2x4 slice. The times are simulated.
32 devices in a mesh: pa: 16 (over z, y, core), pb: 2 (over x).
Axes of the slice: x: 2, y: 2, z: 4, core: 2. Of those that a mesh axis runs over, the one named last changes fastest.
Arguments:
- sources: float32 [4096, 128], P(('pa', 'pb')), may hold values from -3 to 3, as said below
- targets: bfloat16 [4096, 128], P(('pa', 'pb')), may hold values from -2 to 2, as said below
- source_mass: float32 [4096], P(('pa', 'pb')), may hold values from -1 to 1
- target_mass: float32 [4096], P(('pa', 'pb')), may hold values from -1 to 1
Outputs:
- moved: float32 [4096, 128], P(('pa', 'pb'))
- dual_source: float32 [4096], P(('pa', 'pb'))
- dual_target: float32 [4096], P(('pa', 'pb'))
Inputs may be any that keep to these rules, and one draw needn't show every extreme that they name: `targets`: each block of 128 target rows is drawn around one cluster centre, a different one for each block. `sources`: each block of 128 source rows is drawn around a cluster centre of its own, drawn independently of the target centres, possibly offset by a common shift.
All inputs are finite; a program needn't handle non-finite values.
Results may differ from a plain program's by a relative error of at most 0.003.
Values may be sent and summed in bfloat16 or wider, within the bound.
A program may use at most 64 MiB of HBM per device.

v0:
```python
from functools import partial
import jax
import jax.numpy as jnp
from jax import lax
from jax.sharding import PartitionSpec as P

STEPS = 1
ITERS = 2
step_rate = 0.25
floor_value = -1e30


def merged(part, axis, combine):
    gathered = jax.tree.map(lambda a: lax.all_gather(a, axis), part)

    def take(source):
        return jax.tree.map(lambda a: lax.dynamic_index_in_dim(a, source, 0, False), gathered)

    return lax.fori_loop(
        1, lax.axis_size(axis), lambda source, state: combine(state, take(source)), take(0)
    )


def squares(coords):
    wide = coords.astype(jnp.float32)
    return jnp.sum(wide * wide, axis=1)


def pair_cost(left, left_norm, right, right_norm):
    inner = lax.dot_general(
        left, right, (((1,), (1,)), ((), ())), preferred_element_type=jnp.float32
    )
    return left_norm[:, None] + right_norm[None, :] - 2.0 * inner


def over_blocks(update, carry, total):
    block_width = 512 if total % 512 == 0 else total
    block_count = total // block_width
    if block_count == 1:
        return update(carry, 0, block_width)
    return lax.fori_loop(
        0,
        block_count,
        lambda position, current: update(current, position * block_width, block_width),
        carry,
    )


def lse_piece(rows, row_norm, columns, column_norm, carry, piece, start):

    def update(current, offset, length):
        chosen = lax.dynamic_slice_in_dim(columns, start + offset, length, 0)
        chosen_norm = lax.dynamic_slice_in_dim(column_norm, start + offset, length, 0)
        values = lax.dynamic_slice_in_dim(piece, offset, length, 0)
        scores = values[None, :] - pair_cost(rows, row_norm, chosen, chosen_norm)
        highest, totals = current
        raised = jnp.maximum(highest, jnp.max(scores, axis=1))
        totals = totals * jnp.exp(highest - raised) + jnp.sum(
            jnp.exp(scores - raised[:, None]), axis=1
        )
        return (raised, totals)

    return over_blocks(update, carry, piece.shape[0])


def plan_piece(rows, row_norm, row_pot, columns, column_norm, carry, piece, start):

    def update(current, offset, length):
        chosen = lax.dynamic_slice_in_dim(columns, start + offset, length, 0)
        chosen_norm = lax.dynamic_slice_in_dim(column_norm, start + offset, length, 0)
        values = lax.dynamic_slice_in_dim(piece, offset, length, 0)
        cost = pair_cost(rows, row_norm, chosen, chosen_norm)
        weights = jnp.exp(row_pot[:, None] + values[None, :] - cost).astype(jnp.bfloat16)
        return current + jnp.dot(weights, chosen, preferred_element_type=jnp.float32)

    return over_blocks(update, carry, piece.shape[0])


def join_lse(first, second):
    raised = jnp.maximum(first[0], second[0])
    return (raised, first[1] * jnp.exp(first[0] - raised) + second[1] * jnp.exp(second[0] - raised))


def start_lse(length):
    return (jnp.full((length,), floor_value, jnp.float32), jnp.zeros((length,), jnp.float32))


def finish(carry):
    return -(carry[0] + jnp.log(carry[1]))


def body(sources, targets, source_mass, target_mass):
    own_rows = sources.shape[0]
    own_targets = targets.shape[0]
    target_norm = squares(targets)
    moving = sources
    dual_target = jnp.zeros((own_targets,), jnp.float32)
    dual_source = jnp.zeros((own_rows,), jnp.float32)
    member = lax.axis_index("pb")
    half_targets = lax.all_gather(targets, "pa", axis=0, tiled=True)
    half_norm = squares(half_targets)
    pair_mass = lax.all_gather(source_mass, "pb", axis=0, tiled=True)
    pair_dual = jnp.zeros((pair_mass.shape[0],), jnp.float32)
    for flow_step in range(STEPS):
        coarse = moving.astype(jnp.bfloat16)
        pair_coarse = lax.all_gather(coarse, "pb", axis=0, tiled=True)
        pair_norm = squares(pair_coarse)
        pair_count = pair_coarse.shape[0]
        all_sources = lax.all_gather(pair_coarse, "pa", axis=0, tiled=True)
        all_source_norm = squares(all_sources)
        row_fold = partial(lse_piece, pair_coarse, pair_norm, half_targets, half_norm)
        column_fold = partial(lse_piece, targets, target_norm, all_sources, all_source_norm)
        shifted = dual_target + target_mass
        for sweep in range(ITERS + 1):
            shifted = dual_target + target_mass
            half_lse = row_fold(
                start_lse(pair_count),
                jax.tree.map(lambda part: lax.all_gather(part, "pa", axis=0, tiled=True), shifted),
                jnp.int32(0),
            )
            pair_dual = finish(merged((half_lse[0], half_lse[1]), "pb", join_lse))
            if sweep < ITERS:
                lifted = pair_dual + pair_mass
                dual_target = finish(
                    column_fold(
                        start_lse(own_targets),
                        jax.tree.map(
                            lambda part: lax.all_gather(part, "pa", axis=0, tiled=True), lifted
                        ),
                        jnp.int32(0),
                    )
                )
        plan_fold = partial(plan_piece, pair_coarse, pair_norm, pair_dual, half_targets, half_norm)
        empty = jnp.zeros((pair_count, sources.shape[1]), jnp.float32)
        pair_centre = plan_fold(
            empty,
            jax.tree.map(lambda part: lax.all_gather(part, "pa", axis=0, tiled=True), shifted),
            jnp.int32(0),
        )
        centre = lax.psum_scatter(
            pair_centre.astype(jnp.bfloat16), "pb", scatter_dimension=0, tiled=True
        ).astype(jnp.float32)
        moving = moving - 2.0 * step_rate * (moving - centre)
    dual_source = lax.dynamic_slice_in_dim(pair_dual, member * own_rows, own_rows, 0)
    return (moving, dual_source, dual_target)


def solution(mesh):
    return jax.shard_map(
        body,
        mesh=mesh,
        in_specs=(P(("pa", "pb"), None), P(("pa", "pb"), None), P(("pa", "pb")), P(("pa", "pb"))),
        out_specs=(P(("pa", "pb"), None), P(("pa", "pb")), P(("pa", "pb"))),
        check_vma=False,
    )
```

profile of v0, /device:TPU:0, one launch (start us, length us, event | category | flops | bytes accessed | tf_op | source)
XLA Modules:
  0.0 212.0 jit_solution(4313513718906820735)
XLA Ops:
  7.2 0.8 convert_element_type.28
  8.1 5.6 %all_gather.65 = bf16[256,128]{1,0:T(8,128)(2,1)} all-gather(bf16[128,128]{1,0:T(8,128)(2,1)S(1)} %convert_element_type.28), channel_id=1, replica_groups=mesh['pa'=16,'pb'=2] {'pb'}, dimensions={0}, use_global_device_ids=true | all-gather | bytes 98304 | tf_op jit(solution)/shard_map/all_gather | solution.py:106
  13.7 1.0 multiply_reduce_fusion.2
  14.7 24.4 %all_gather.66 = bf16[2048,128]{1,0:T(8,128)(2,1)S(1)} all-gather(bf16[128,128]{1,0:T(8,128)(2,1)} %param.17), channel_id=1, replica_groups=mesh['pa'=16,'pb'=2] {'pa'}, dimensions={0}, use_global_device_ids=true | all-gather | bytes 557056 | tf_op jit(solution)/shard_map/all_gather | solution.py:100
  39.1 0.3 multiply_reduce_fusion.1
  39.4 17.5 %all-gather.6 = f32[16,1,128]{2,1,0:T(1,128)S(1)} all-gather(f32[1,1,128]{2,1,0:T(1,128)S(1)} %bitcast.107), channel_id=1, replica_groups=mesh['pa'=16,'pb'=2] {'pa'}, dimensions={0}, use_global_device_ids=true | all-gather | bytes 8704 | tf_op jit(solution)/shard_map/all_gather | solution.py:118
  56.9 2.4 %while.112 = (s32[]{:T(128)}, f32[256]{0:T(256)S(1)}, f32[256]{0:T(256)S(1)}, f32[2048]{0:T(1024)S(1)}, f32[256]{0:T(256)S(1)}, /*index=5*/f32[2048]{0:T(1024)S(...) while((s32[]{:T(128)}, f32[256]{0:T(256)S(1)}, ...), condition=%wide.region_6.7_spmd.clone, body=%wide.region_3.6_spmd.clone.sunk | while | flops 34473220 | bytes 1271994 | solution.py:41
  57.1 0.3 fusion.104
  57.4 0.1 exponential_reduce_fusion.10
  57.7 0.3 fusion.104
  58.0 0.1 exponential_reduce_fusion.10
  58.3 0.3 fusion.104
  58.9 0.3 fusion.104
  59.4 4.2 %all-gather.9 = f32[2,1,128]{2,1,0:T(1,128)S(1)} all-gather(f32[1,1,128]{2,1,0:T(1,128)S(1)} %bitcast.124), channel_id=1, replica_groups=mesh['pa'=16,'pb'=2] {'pb'}, dimensions={0}, use_global_device_ids=true | all-gather | bytes 1536 | tf_op jit(solution)/shard_map/all_gather | solution.py:102
  63.7 4.2 %all-gather.7 = f32[2,1,256]{2,1,0:T(1,128)S(1)} all-gather(f32[1,1,256]{2,1,0:T(1,128)S(1)} %bitcast.98), channel_id=2, replica_groups=mesh['pa'=16,'pb'=2] {'pb'}, dimensions={0}, use_global_device_ids=true | all-gather | bytes 3072 | tf_op jit(solution)/shard_map/all_gather | solution.py:14
  67.9 4.2 %all-gather.8 = f32[2,1,256]{2,1,0:T(1,128)S(1)} all-gather(f32[1,1,256]{2,1,0:T(1,128)S(1)} %bitcast.106), channel_id=3, replica_groups=mesh['pa'=16,'pb'=2] {'pb'}, dimensions={0}, use_global_device_ids=true | all-gather | bytes 3072 | tf_op jit(solution)/shard_map/all_gather | solution.py:14
  72.2 18.8 %all-gather.10 = f32[16,1,256]{2,1,0:T(1,128)S(1)} all-gather(f32[1,1,256]{2,1,0:T(1,128)S(1)} %bitcast.113), channel_id=1, replica_groups=mesh['pa'=16,'pb'=2] {'pa'}, dimensions={0}, use_global_device_ids=true | all-gather | bytes 17408 | tf_op jit(solution)/shard_map/all_gather | solution.py:128
  91.2 1.8 multiply_reduce_fusion
  93.0 11.5 %while.113 = (s32[]{:T(128)}, f32[128]{0:T(128)S(1)}, f32[128]{0:T(128)S(1)}, f32[4096]{0:T(1024)S(1)}, f32[128]{0:T(128)S(1)}, /*index=5*/f32[4096]{0:T(1024)S(...) while((s32[]{:T(128)}, f32[128]{0:T(128)S(1)}, ...), condition=%wide.region_11.0_spmd.clone, body=%wide.region_8.11_spmd.clone.sunk | while | flops 17236612 | bytes 707770 | solution.py:41
  93.2 1.1 fusion.108
  94.6 1.1 fusion.108
  96.1 1.1 fusion.108
  97.5 1.1 fusion.108
  98.9 1.1 fusion.108
  100.4 1.1 fusion.108
  101.8 1.1 fusion.108
  103.3 1.1 fusion.108
  104.6 17.4 %all-gather.11 = f32[16,1,128]{2,1,0:T(1,128)S(1)} all-gather(f32[1,1,128]{2,1,0:T(1,128)S(1)} %add_bitcast_fusion.1), channel_id=1, replica_groups=mesh['pa'=16,'pb'=2] {'pa'}, dimensions={0}, use_global_device_ids=true | all-gather | bytes 8704 | tf_op jit(solution)/shard_map/all_gather | solution.py:118
  122.0 2.4 %while.114 = (s32[]{:T(128)}, f32[256]{0:T(256)S(1)}, f32[256]{0:T(256)S(1)}, f32[2048]{0:T(1024)S(1)}, f32[256]{0:T(256)S(1)}, /*index=5*/f32[2048]{0:T(1024)S(...) while((s32[]{:T(128)}, f32[256]{0:T(256)S(1)}, ...), condition=%wide.region_15.0_spmd.clone, body=%wide.region_12.15_spmd.clone.sunk | while | flops 34473220 | bytes 1271994 | solution.py:41
  122.2 0.3 fusion.112
  122.8 0.3 fusion.112
  123.4 0.3 fusion.112
  124.0 0.3 fusion.112
  124.4 4.2 %all-gather.12 = f32[2,1,256]{2,1,0:T(1,128)S(1)} all-gather(f32[1,1,256]{2,1,0:T(1,128)S(1)} %bitcast.97), channel_id=4, replica_groups=mesh['pa'=16,'pb'=2] {'pb'}, dimensions={0}, use_global_device_ids=true | all-gather | bytes 3072 | tf_op jit(solution)/shard_map/all_gather | solution.py:14
  128.7 4.2 %all-gather.13 = f32[2,1,256]{2,1,0:T(1,128)S(1)} all-gather(f32[1,1,256]{2,1,0:T(1,128)S(1)} %bitcast.105), channel_id=5, replica_groups=mesh['pa'=16,'pb'=2] {'pb'}, dimensions={0}, use_global_device_ids=true | all-gather | bytes 3072 | tf_op jit(solution)/shard_map/all_gather | solution.py:14
  132.9 18.8 %all-gather.14 = f32[16,1,256]{2,1,0:T(1,128)S(1)} all-gather(f32[1,1,256]{2,1,0:T(1,128)S(1)} %bitcast.112), channel_id=1, replica_groups=mesh['pa'=16,'pb'=2] {'pa'}, dimensions={0}, use_global_device_ids=true | all-gather | bytes 17408 | tf_op jit(solution)/shard_map/all_gather | solution.py:128
  151.7 11.5 %while.115 = (s32[]{:T(128)}, f32[128]{0:T(128)S(1)}, f32[128]{0:T(128)S(1)}, f32[4096]{0:T(1024)S(1)}, f32[128]{0:T(128)S(1)}, /*index=5*/f32[4096]{0:T(1024)S(...) while((s32[]{:T(128)}, f32[128]{0:T(128)S(1)}, ...), condition=%wide.region_19.20_spmd.clone, body=%wide.region_16.19_spmd.clone.sunk | while | flops 17236612 | bytes 707770 | solution.py:41
  151.9 1.1 fusion.116
  153.3 1.1 fusion.116
  154.8 1.1 fusion.116
  156.2 1.1 fusion.116
  157.6 1.1 fusion.116
  159.1 1.1 fusion.116
  160.5 1.1 fusion.116
  162.0 1.1 fusion.116
  163.3 0.5 add_bitcast_fusion
  163.8 17.4 %all-gather.15 = f32[16,1,128]{2,1,0:T(1,128)S(1)} all-gather(f32[1,1,128]{2,1,0:T(1,128)S(1)} %get-tuple-element.1165), channel_id=1, replica_groups=mesh['pa'=16,'pb'=2] {'pa'}, dimensions={0}, use_global_device_ids=true | all-gather | bytes 8704 | tf_op jit(solution)/shard_map/all_gather | solution.py:137
  181.2 2.4 %while.116 = (s32[]{:T(128)}, f32[256]{0:T(256)S(1)}, f32[256]{0:T(256)S(1)}, f32[2048]{0:T(1024)S(1)}, f32[256]{0:T(256)S(1)}, /*index=5*/f32[2048]{0:T(1024)S(...) while((s32[]{:T(128)}, f32[256]{0:T(256)S(1)}, ...), condition=%wide.region_23.24_spmd.clone, body=%wide.region_20.23_spmd.clone.sunk | while | flops 34473220 | bytes 1271994 | solution.py:41
  181.4 0.3 fusion.120
  182.0 0.3 fusion.120
  182.3 0.1 exponential_reduce_fusion.14
  182.6 0.3 fusion.120
  183.2 0.3 fusion.120
  183.6 4.2 %all-gather.16 = f32[2,1,256]{2,1,0:T(1,128)S(1)} all-gather(f32[1,1,256]{2,1,0:T(1,128)S(1)} %bitcast.96), channel_id=6, replica_groups=mesh['pa'=16,'pb'=2] {'pb'}, dimensions={0}, use_global_device_ids=true | all-gather | bytes 3072 | tf_op jit(solution)/shard_map/all_gather | solution.py:14
  187.9 4.2 %all-gather.17 = f32[2,1,256]{2,1,0:T(1,128)S(1)} all-gather(f32[1,1,256]{2,1,0:T(1,128)S(1)} %bitcast.104), channel_id=7, replica_groups=mesh['pa'=16,'pb'=2] {'pb'}, dimensions={0}, use_global_device_ids=true | all-gather | bytes 3072 | tf_op jit(solution)/shard_map/all_gather | solution.py:14
  192.1 2.4 %while.117 = (s32[]{:T(128)}, f32[256,128]{1,0:T(8,128)S(1)}, f32[256]{0:T(256)S(1)}, f32[2048]{0:T(1024)S(1)}, f32[256]{0:T(256)S(1)}, /*index=5*/f32[2048]{0:T...) while((s32[]{:T(128)}, f32[256,128]{1,0:T(8,128)S(1)}, ...), condition=%wide.region_25.0_spmd.clone, body=%wide.region_24.25_spmd.clone.sunk | while | flops 67960840 | bytes 605876 | solution.py:41
  192.3 0.4 fusion.126
  192.9 0.4 fusion.126
  193.5 0.4 fusion.126
  194.1 0.4 fusion.126
  194.5 0.6 convert_element_type.33
  195.2 0.6 dynamic_slice.184
  195.8 8.0 %reduce-scatter.2.cloned.1.call-done = bf16[128,128]{1,0:T(8,128)(2,1)} async-done(((bf16[256,128]{1,0:T(8,128)(2,1)}), bf16[128,128]{1,0:T(8,128)(2,1)}) %reduce-scatter.2.cloned.1.call-update) | async-done | bytes 32784 | tf_op jit(solution)/shard_map/reduce_scatter | solution.py:140
  203.7 1.4 multiply_subtract_fusion
  (210 shorter events, 8.5 us)
Async XLA Ops:
  7.2 32.3 %copy-start.3 = (f32[128]{0:T(128)S(1)}, f32[128]{0:T(128)}, u32[]{:S(2)}) copy-start(f32[128]{0:T(128)} %param.19) | copy-start | bytes 1540
  7.2 84.0 %all-gather.20.cloned.1.call-start = ((), (), s32[]{:S(2)}) async-start(), calls=%async_computation.1 | async-start | bytes 1114112 | tf_op jit(solution)/shard_map/all_gather | solution.py:109
  13.7 43.2 %copy-start = (bf16[256,128]{1,0:T(8,128)(2,1)S(1)}, bf16[256,128]{1,0:T(8,128)(2,1)}, u32[]{:S(2)}) copy-start(bf16[256,128]{1,0:T(8,128)(2,1)} %all_gather.65) | copy-start | bytes 196612
  13.7 190.0 %reduce-scatter.2.cloned.1.call-start = ((), (), s32[]{:S(2)}) async-start(), calls=%async_computation.2 | async-start | bytes 98304 | tf_op jit(solution)/shard_map/reduce_scatter | solution.py:140
  56.9 2.5 %copy-start.4 = (f32[128]{0:T(128)S(1)}, f32[128]{0:T(128)}, u32[]{:S(2)}) copy-start(f32[128]{0:T(128)} %param.18) | copy-start | bytes 1540
  56.9 34.1 %copy-start.2 = (bf16[128,128]{1,0:T(8,128)(2,1)S(1)}, bf16[128,128]{1,0:T(8,128)(2,1)}, u32[]{:S(2)}) copy-start(bf16[128,128]{1,0:T(8,128)(2,1)} %param.17) | copy-start | bytes 98308
  192.1 11.6 %copy-start.1 = (f32[128,128]{1,0:T(8,128)S(1)}, f32[128,128]{1,0:T(8,128)}, u32[]{:S(2)}) copy-start(f32[128,128]{1,0:T(8,128)} %param.16) | copy-start | bytes 196612
Sparse Core Ops, SparseCore 0:
  13.8 40.4 all-gather.19
  195.3 8.3 reduce-scatter.1
where the time goes:
time: 213 us; the launch traced here: 212 us
  blocking collectives  150 us (70%)
  matrix products  23.1 us (11%)
  between operations  14.3 us (7%)
  other arithmetic  10.3 us (5%)
  waiting for transfers between devices  8.02 us (4%)
  local copies, waits for them, and re-layouts  5.52 us (3%)
    all_gather x5, blocking collectives, body(): lax.all_gather(part, 'pa', axis=0, tiled=True)  90 us
    all_gather x6, blocking collectives, merged(): gathered = jax.tree.map(lambda a: lax.all_gather(a, axis), part)  25.4 us
    all_gather x1, blocking collectives, body(): half_targets = lax.all_gather(targets, 'pa', axis=0, tiled=True)  24.4 us
    dot_general x28, matrix products, pair_cost(): lax.dot_general(left, right, (((1,), (1,)), ((), ())), preferred_element_...  21.5 us
    reduce_scatter x1, waiting for transfers between devices, body(): lax.psum_scatter(pair_centre.astype(jnp.bfloat16), 'pb', scatter_dimensio...  7.97 us
    all_gather x1, blocking collectives, body(): pair_coarse = lax.all_gather(coarse, 'pb', axis=0, tiled=True)  5.6 us
  transfers between devices with their start and end apart: 2, of which 1 were waited for; matrix products, arithmetic and copies ran while one was open for 2% of the time, Pallas kernels for 0%

commit v1 on v0

--- a/solution.py
+++ b/solution.py
@@ -1,3 +1,4 @@
+import functools
 from functools import partial
 import jax
 import jax.numpy as jnp
@@ -8,6 +9,21 @@
 ITERS = 2
 step_rate = 0.25
 floor_value = -1e30
+
+
+def unite_spots(slab_in, row_dim):
+    return jnp.concatenate(
+        lax.all_to_all(
+            jnp.stack([slab_in] * lax.axis_size("pa"), 0),
+            axis_name="pa",
+            concat_axis=0,
+            split_axis=0,
+        ),
+        row_dim,
+    )
+
+
+lane_push = functools.partial(unite_spots, row_dim=0)
 
 
 def merged(part, axis, combine):
@@ -97,7 +113,7 @@
     dual_target = jnp.zeros((own_targets,), jnp.float32)
     dual_source = jnp.zeros((own_rows,), jnp.float32)
     member = lax.axis_index("pb")
-    half_targets = lax.all_gather(targets, "pa", axis=0, tiled=True)
+    half_targets = lane_push(targets)
     half_norm = squares(half_targets)
     pair_mass = lax.all_gather(source_mass, "pb", axis=0, tiled=True)
     pair_dual = jnp.zeros((pair_mass.shape[0],), jnp.float32)

time: 213 us -> 203 us (0.953)
  blocking collectives: 150 us -> 129 us
  starting transfers between devices: 0.08 us -> 7.5 us
  matrix products: 23.1 us -> 26.5 us
    all_gather x1 -> x0, blocking collectives: 24.4 us -> none  [body(): half_targets = lax.all_gather(targets, 'pa', axis=0, tiled=True)]
    all_to_all x0 -> x1, starting transfers between devices: none -> 7.41 us  [unite_spots(): lax.all_to_all(jnp.stack([slab_in] * lax.axis_size('pa'), 0), axis_name='...]
    all_gather x5, blocking collectives: 90 us -> 94.2 us  [body(): lax.all_gather(part, 'pa', axis=0, tiled=True)]
    dot_general x28, matrix products: 21.5 us -> 24.9 us  [pair_cost(): lax.dot_general(left, right, (((1,), (1,)), ((), ())), preferred_element_...]
  transfers between devices with their start and end apart: 2 -> 3, of which waited for: 1 -> 1; matrix products, arithmetic and copies ran while one was open for 2% -> 4% of each run, Pallas kernels for 0% -> 0%
where the time goes in v1:
time: 203 us; the launch traced here: 202 us
  blocking collectives  129 us (64%)
  matrix products  26.5 us (13%)
  between operations  14.3 us (7%)
  other arithmetic  9.48 us (5%)
  starting transfers between devices  7.5 us (4%)
  local copies, waits for them, and re-layouts  7.23 us (4%)
  waiting for transfers between devices  6.86 us (3%)
    all_gather x5, blocking collectives, body(): lax.all_gather(part, 'pa', axis=0, tiled=True)  94.2 us
    all_gather x6, blocking collectives, merged(): gathered = jax.tree.map(lambda a: lax.all_gather(a, axis), part)  25.4 us
    dot_general x28, matrix products, pair_cost(): lax.dot_general(left, right, (((1,), (1,)), ((), ())), preferred_element_...  24.9 us
    all_to_all x1, starting transfers between devices, unite_spots(): lax.all_to_all(jnp.stack([slab_in] * lax.axis_size('pa'), 0), axis_name='...  7.41 us
    reduce_scatter x1, waiting for transfers between devices, body(): lax.psum_scatter(pair_centre.astype(jnp.bfloat16), 'pb', scatter_dimensio...  6.82 us
    all_gather x1, blocking collectives, body(): pair_coarse = lax.all_gather(coarse, 'pb', axis=0, tiled=True)  4.69 us
    all_gather x1, blocking collectives, body(): pair_mass = lax.all_gather(source_mass, 'pb', axis=0, tiled=True)  4.24 us
  transfers between devices with their start and end apart: 3, of which 1 were waited for; matrix products, arithmetic and copies ran while one was open for 4% of the time, Pallas kernels for 0%

profile of v1, /device:TPU:0, one launch (start us, length us, event | category | flops | bytes accessed | tf_op | source)
XLA Modules:
  0.0 201.5 jit_solution(14986865541327384486)
XLA Ops:
  7.2 1.7 stack.2
  8.9 7.4 %all-to-all-start = ((bf16[16,128,128]{2,1,0:T(8,128)(2,1)}), bf16[16,128,128]{2,1,0:T(8,128)(2,1)S(1)}, u32[]{:S(2)}, u32[]{:S(2)}) async-start(bf16[16,128,128]{2,1,0:T(8,128)(2,1)} %stack.2), calls=%async_computation | async-start | bytes 1048576 | tf_op jit(solution)/shard_map/all_to_all | solution.py:16
  16.4 4.7 %all_gather.62 = bf16[256,128]{1,0:T(8,128)(2,1)} all-gather(bf16[128,128]{1,0:T(8,128)(2,1)S(1)} %convert_element_type.29), channel_id=1, replica_groups=mesh['pa'=16,'pb'=2] {'pb'}, dimensions={0}, use_global_device_ids=true | all-gather | bytes 98304 | tf_op jit(solution)/shard_map/all_gather | solution.py:122
  21.3 4.2 %all-gather.9 = f32[2,1,128]{2,1,0:T(1,128)S(1)} all-gather(f32[1,1,128]{2,1,0:T(1,128)S(1)} %bitcast.128), channel_id=1, replica_groups=mesh['pa'=16,'pb'=2] {'pb'}, dimensions={0}, use_global_device_ids=true | all-gather | bytes 1536 | tf_op jit(solution)/shard_map/all_gather | solution.py:118
  25.5 21.7 %all-gather.6 = f32[16,1,128]{2,1,0:T(1,128)S(1)} all-gather(f32[1,1,128]{2,1,0:T(1,128)S(1)} %bitcast.111), channel_id=1, replica_groups=mesh['pa'=16,'pb'=2] {'pa'}, dimensions={0}, use_global_device_ids=true | all-gather | bytes 8704 | tf_op jit(solution)/shard_map/all_gather | solution.py:134
  47.4 1.0 multiply_reduce_fusion.2
  48.3 0.3 multiply_reduce_fusion.1
  48.7 5.8 %while.112 = (s32[]{:T(128)}, f32[256]{0:T(256)S(1)}, f32[256]{0:T(256)S(1)}, f32[2048]{0:T(1024)S(1)}, f32[256]{0:T(256)S(1)}, /*index=5*/f32[2048]{0:T(1024)S(...) while((s32[]{:T(128)}, f32[256]{0:T(256)S(1)}, ...), condition=%wide.region_6.7_spmd.clone, body=%wide.region_3.6_spmd.clone.sunk | while | flops 34473220 | bytes 1271994 | solution.py:57
  48.9 1.1 fusion.104
  50.3 1.1 fusion.104
  51.8 1.1 fusion.104
  53.2 1.1 fusion.104
  54.5 4.2 %all-gather.7 = f32[2,1,256]{2,1,0:T(1,128)S(1)} all-gather(f32[1,1,256]{2,1,0:T(1,128)S(1)} %bitcast.102), channel_id=2, replica_groups=mesh['pa'=16,'pb'=2] {'pb'}, dimensions={0}, use_global_device_ids=true | all-gather | bytes 3072 | tf_op jit(solution)/shard_map/all_gather | solution.py:30
  58.7 4.2 %all-gather.8 = f32[2,1,256]{2,1,0:T(1,128)S(1)} all-gather(f32[1,1,256]{2,1,0:T(1,128)S(1)} %bitcast.110), channel_id=3, replica_groups=mesh['pa'=16,'pb'=2] {'pb'}, dimensions={0}, use_global_device_ids=true | all-gather | bytes 3072 | tf_op jit(solution)/shard_map/all_gather | solution.py:30
  63.0 17.2 %all-gather.10 = f32[16,1,256]{2,1,0:T(1,128)S(1)} all-gather(f32[1,1,256]{2,1,0:T(1,128)S(1)} %bitcast.117), channel_id=1, replica_groups=mesh['pa'=16,'pb'=2] {'pa'}, dimensions={0}, use_global_device_ids=true | all-gather | bytes 17408 | tf_op jit(solution)/shard_map/all_gather | solution.py:144
  80.2 1.8 multiply_reduce_fusion
  82.0 11.5 %while.113 = (s32[]{:T(128)}, f32[128]{0:T(128)S(1)}, f32[128]{0:T(128)S(1)}, f32[4096]{0:T(1024)S(1)}, f32[128]{0:T(128)S(1)}, /*index=5*/f32[4096]{0:T(1024)S(...) while((s32[]{:T(128)}, f32[128]{0:T(128)S(1)}, ...), condition=%wide.region_11.0_spmd.clone, body=%wide.region_8.11_spmd.clone.sunk | while | flops 17236612 | bytes 707770 | solution.py:57
  82.2 1.1 fusion.108
  83.6 1.1 fusion.108
  85.1 1.1 fusion.108
  86.5 1.1 fusion.108
  88.0 1.1 fusion.108
  89.4 1.1 fusion.108
  90.8 1.1 fusion.108
  92.3 1.1 fusion.108
  93.6 19.1 %all-gather.11 = f32[16,1,128]{2,1,0:T(1,128)S(1)} all-gather(f32[1,1,128]{2,1,0:T(1,128)S(1)} %add_bitcast_fusion.1), channel_id=1, replica_groups=mesh['pa'=16,'pb'=2] {'pa'}, dimensions={0}, use_global_device_ids=true | all-gather | bytes 8704 | tf_op jit(solution)/shard_map/all_gather | solution.py:134
  112.7 2.4 %while.114 = (s32[]{:T(128)}, f32[256]{0:T(256)S(1)}, f32[256]{0:T(256)S(1)}, f32[2048]{0:T(1024)S(1)}, f32[256]{0:T(256)S(1)}, /*index=5*/f32[2048]{0:T(1024)S(...) while((s32[]{:T(128)}, f32[256]{0:T(256)S(1)}, ...), condition=%wide.region_15.0_spmd.clone, body=%wide.region_12.15_spmd.clone.sunk | while | flops 34473220 | bytes 1271994 | solution.py:57
  112.8 0.3 fusion.112
  113.4 0.3 fusion.112
  114.0 0.3 fusion.112
  114.7 0.3 fusion.112
  115.1 4.2 %all-gather.12 = f32[2,1,256]{2,1,0:T(1,128)S(1)} all-gather(f32[1,1,256]{2,1,0:T(1,128)S(1)} %bitcast.101), channel_id=4, replica_groups=mesh['pa'=16,'pb'=2] {'pb'}, dimensions={0}, use_global_device_ids=true | all-gather | bytes 3072 | tf_op jit(solution)/shard_map/all_gather | solution.py:30
  119.3 4.2 %all-gather.13 = f32[2,1,256]{2,1,0:T(1,128)S(1)} all-gather(f32[1,1,256]{2,1,0:T(1,128)S(1)} %bitcast.109), channel_id=5, replica_groups=mesh['pa'=16,'pb'=2] {'pb'}, dimensions={0}, use_global_device_ids=true | all-gather | bytes 3072 | tf_op jit(solution)/shard_map/all_gather | solution.py:30
  123.6 17.2 %all-gather.14 = f32[16,1,256]{2,1,0:T(1,128)S(1)} all-gather(f32[1,1,256]{2,1,0:T(1,128)S(1)} %bitcast.116), channel_id=1, replica_groups=mesh['pa'=16,'pb'=2] {'pa'}, dimensions={0}, use_global_device_ids=true | all-gather | bytes 17408 | tf_op jit(solution)/shard_map/all_gather | solution.py:144
  140.8 11.5 %while.115 = (s32[]{:T(128)}, f32[128]{0:T(128)S(1)}, f32[128]{0:T(128)S(1)}, f32[4096]{0:T(1024)S(1)}, f32[128]{0:T(128)S(1)}, /*index=5*/f32[4096]{0:T(1024)S(...) while((s32[]{:T(128)}, f32[128]{0:T(128)S(1)}, ...), condition=%wide.region_19.20_spmd.clone, body=%wide.region_16.19_spmd.clone.sunk | while | flops 17236612 | bytes 707770 | solution.py:57
  140.9 1.1 fusion.116
  142.4 1.1 fusion.116
  143.8 1.1 fusion.116
  145.2 1.1 fusion.116
  146.7 1.1 fusion.116
  148.1 1.1 fusion.116
  149.6 1.1 fusion.116
  151.0 1.1 fusion.116
  152.3 0.5 add_bitcast_fusion
  152.8 19.1 %all-gather.15 = f32[16,1,128]{2,1,0:T(1,128)S(1)} all-gather(f32[1,1,128]{2,1,0:T(1,128)S(1)} %get-tuple-element.1165), channel_id=1, replica_groups=mesh['pa'=16,'pb'=2] {'pa'}, dimensions={0}, use_global_device_ids=true | all-gather | bytes 8704 | tf_op jit(solution)/shard_map/all_gather | solution.py:153
  171.9 2.4 %while.116 = (s32[]{:T(128)}, f32[256]{0:T(256)S(1)}, f32[256]{0:T(256)S(1)}, f32[2048]{0:T(1024)S(1)}, f32[256]{0:T(256)S(1)}, /*index=5*/f32[2048]{0:T(1024)S(...) while((s32[]{:T(128)}, f32[256]{0:T(256)S(1)}, ...), condition=%wide.region_23.24_spmd.clone, body=%wide.region_20.23_spmd.clone.sunk | while | flops 34473220 | bytes 1271994 | solution.py:57
  172.0 0.3 fusion.120
  172.3 0.1 exponential_reduce_fusion.14
  172.6 0.3 fusion.120
  173.2 0.3 fusion.120
  173.5 0.1 exponential_reduce_fusion.14
  173.9 0.3 fusion.120
  174.1 0.1 exponential_reduce_fusion.14
  174.3 4.2 %all-gather.16 = f32[2,1,256]{2,1,0:T(1,128)S(1)} all-gather(f32[1,1,256]{2,1,0:T(1,128)S(1)} %bitcast.100), channel_id=6, replica_groups=mesh['pa'=16,'pb'=2] {'pb'}, dimensions={0}, use_global_device_ids=true | all-gather | bytes 3072 | tf_op jit(solution)/shard_map/all_gather | solution.py:30
  178.5 4.2 %all-gather.17 = f32[2,1,256]{2,1,0:T(1,128)S(1)} all-gather(f32[1,1,256]{2,1,0:T(1,128)S(1)} %bitcast.108), channel_id=7, replica_groups=mesh['pa'=16,'pb'=2] {'pb'}, dimensions={0}, use_global_device_ids=true | all-gather | bytes 3072 | tf_op jit(solution)/shard_map/all_gather | solution.py:30
  182.8 2.4 %while.117 = (s32[]{:T(128)}, f32[256,128]{1,0:T(8,128)S(1)}, f32[256]{0:T(256)S(1)}, f32[2048]{0:T(1024)S(1)}, f32[256]{0:T(256)S(1)}, /*index=5*/f32[2048]{0:T...) while((s32[]{:T(128)}, f32[256,128]{1,0:T(8,128)S(1)}, ...), condition=%wide.region_25.0_spmd.clone, body=%wide.region_24.25_spmd.clone.sunk | while | flops 67960840 | bytes 605876 | solution.py:57
  183.0 0.4 fusion.126
  183.6 0.4 fusion.126
  184.2 0.4 fusion.126
  184.8 0.4 fusion.126
  185.2 0.6 convert_element_type.34
  185.9 0.6 dynamic_slice.184
  186.4 6.8 %reduce-scatter.2.cloned.1.call-done = bf16[128,128]{1,0:T(8,128)(2,1)} async-done(((bf16[256,128]{1,0:T(8,128)(2,1)}), bf16[128,128]{1,0:T(8,128)(2,1)}) %reduce-scatter.2.cloned.1.call-update) | async-done | bytes 32784 | tf_op jit(solution)/shard_map/reduce_scatter | solution.py:156
  193.3 1.4 multiply_subtract_fusion
  (212 shorter events, 8.5 us)
Async XLA Ops:
  7.2 40.1 %copy-start.2 = (bf16[128,128]{1,0:T(8,128)(2,1)S(1)}, bf16[128,128]{1,0:T(8,128)(2,1)}, u32[]{:S(2)}) copy-start(bf16[128,128]{1,0:T(8,128)(2,1)} %param.17) | copy-start | bytes 98308
  7.2 9.2 %copy-start.1 = (f32[128,128]{1,0:T(8,128)S(1)}, f32[128,128]{1,0:T(8,128)}, u32[]{:S(2)}) copy-start(f32[128,128]{1,0:T(8,128)} %param.16) | copy-start | bytes 196612
  7.2 14.1 %copy-start.4 = (f32[128]{0:T(128)S(1)}, f32[128]{0:T(128)}, u32[]{:S(2)}) copy-start(f32[128]{0:T(128)} %param.18) | copy-start | bytes 1540
  7.2 18.3 %copy-start.3 = (f32[128]{0:T(128)S(1)}, f32[128]{0:T(128)}, u32[]{:S(2)}) copy-start(f32[128]{0:T(128)} %param.19) | copy-start | bytes 1540
  8.9 39.4 %all-to-all-start = ((bf16[16,128,128]{2,1,0:T(8,128)(2,1)}), bf16[16,128,128]{2,1,0:T(8,128)(2,1)S(1)}, u32[]{:S(2)}, u32[]{:S(2)}) async-start(bf16[16,128,128]{2,1,0:T(8,128)(2,1)} %stack.2), calls=%async_computation | async-start | bytes 1048576 | tf_op jit(solution)/shard_map/all_to_all | solution.py:16
  16.3 63.8 %all-gather.20.cloned.1.call-start = ((), (), s32[]{:S(2)}) async-start(), calls=%async_computation.2 | async-start | bytes 1114112 | tf_op jit(solution)/shard_map/all_gather | solution.py:125
  21.1 172.1 %reduce-scatter.2.cloned.1.call-start = ((), (), s32[]{:S(2)}) async-start(), calls=%async_computation.3 | async-start | bytes 98304 | tf_op jit(solution)/shard_map/reduce_scatter | solution.py:156
  82.0 30.7 %copy-start = (bf16[256,128]{1,0:T(8,128)(2,1)S(1)}, bf16[256,128]{1,0:T(8,128)(2,1)}, u32[]{:S(2)}) copy-start(bf16[256,128]{1,0:T(8,128)(2,1)} %get-tuple-element.1729) | copy-start | bytes 196612
Sparse Core Ops, SparseCore 0:
  21.3 39.1 all-gather.19
  186.0 7.2 reduce-scatter.1
